TPU v7x, 32 devices: a whole 2x2x4 slice. The times are simulated.
32 devices in a mesh: dp: 16 (over z, y, x), mp: 2 (over core).
Axes of the slice: x: 2, y: 2, z: 4, core: 2. Of those that a mesh axis runs over, the one named last changes fastest.
Arguments:
- hidden_state: bfloat16 [32, 19, 19, 256], P('dp'), may hold values from -6 to 6
- actions: int32 [32, 2], P('dp'), may hold values from 0 to 361
- value_target: int32 [32, 2], P('dp'), may hold values from 0 to 600
- reward_target: int32 [32, 2], P('dp'), may hold values from 0 to 600
- kernel_first: float32 [3, 3, 256, 256], P(None, None, 'dp', 'mp'), may hold values from -6 to 6
- kernel_second: float32 [3, 3, 256, 256], P(None, None, 'dp', 'mp'), may hold values from -6 to 6
- head_weight: float32 [2, 256, 601], P('mp', 'dp'), may hold values from -6 to 6
- action_embed: float32 [2, 256], P('mp', 'dp'), may hold values from -6 to 6
- first_mean: float32 [3, 3, 256, 256], P(None, None, 'dp', 'mp'), may hold values from -0.00061035156 to 0.00061035156
- first_square: float32 [3, 3, 256, 256], P(None, None, 'dp', 'mp'), may hold values from 1e-09 to 1e-06
- second_mean: float32 [3, 3, 256, 256], P(None, None, 'dp', 'mp'), may hold values from -0.00061035156 to 0.00061035156
- second_square: float32 [3, 3, 256, 256], P(None, None, 'dp', 'mp'), may hold values from 1e-09 to 1e-06
- head_mean: float32 [2, 256, 601], P('mp', 'dp'), may hold values from -0.0029296875 to 0.0029296875
- head_square: float32 [2, 256, 601], P('mp', 'dp'), may hold values from 1e-08 to 1e-06
- embed_mean: float32 [2, 256], P('mp', 'dp'), may hold values from -0.0017089844 to 0.0017089844
- embed_square: float32 [2, 256], P('mp', 'dp'), may hold values from 1e-09 to 1e-06
Outputs:
- kernel_first_new: float32 [3, 3, 256, 256], P(None, None, 'dp', 'mp')
- kernel_second_new: float32 [3, 3, 256, 256], P(None, None, 'dp', 'mp')
- head_weight_new: float32 [2, 256, 601], P('mp', 'dp')
- action_embed_new: float32 [2, 256], P('mp', 'dp')
- first_mean_new: float32 [3, 3, 256, 256], P(None, None, 'dp', 'mp')
- first_square_new: float32 [3, 3, 256, 256], P(None, None, 'dp', 'mp')
- second_mean_new: float32 [3, 3, 256, 256], P(None, None, 'dp', 'mp')
- second_square_new: float32 [3, 3, 256, 256], P(None, None, 'dp', 'mp')
- head_mean_new: float32 [2, 256, 601], P('mp', 'dp')
- head_square_new: float32 [2, 256, 601], P('mp', 'dp')
- embed_mean_new: float32 [2, 256], P('mp', 'dp')
- embed_square_new: float32 [2, 256], P('mp', 'dp')
- first_grad: float32 [3, 3, 256, 256], P(None, None, 'dp', 'mp')
- second_grad: float32 [3, 3, 256, 256], P(None, None, 'dp', 'mp')
- head_grad: float32 [2, 256, 601], P('mp', 'dp')
- embed_grad: float32 [2, 256], P('mp', 'dp')
Inputs may be any that keep to these rules, and one draw needn't show every extreme that they name: `actions`: the value 361 stands for a pass.
All inputs are finite; a program needn't handle non-finite values.
Results may differ from a plain program's by a relative error of at most 0.02.
Values may be sent and summed in bfloat16 or wider, within the bound.
No kernel may reach another device: no remote copies, remote signals or barrier semaphores. Data moves between devices by JAX's collectives and lax.ppermute only.
A program may use at most 64 MiB of HBM per device.

v0:
```python
import jax
import jax.numpy as jnp
from jax import lax
from jax.sharding import PartitionSpec as P

CHANNELS = 256
head_scale = 4.0
soft_cap = 15.0
eps_norm = 1e-05
beta_one = 0.9
beta_two = 0.999
step_size = 0.1
eps_adam = 1e-08


def conv_apply(field, kernel, layout):
    return lax.conv_general_dilated(
        field,
        kernel,
        (1, 1),
        "SAME",
        dimension_numbers=("NHWC", layout, "NHWC"),
        preferred_element_type=jnp.float32,
    )


def gate_slope(pre):
    sig = jax.nn.sigmoid(pre)
    return sig * (1.0 + pre * (1.0 - sig))


def tap_products(field, grad, field_rows):
    side = field.shape[1]
    padded = jnp.pad(field, ((0, 0), (1, 1), (1, 1), (0, 0)))
    flat_grad = grad.reshape(-1, grad.shape[3])
    blocks = []
    for offset in range(9):
        row_start = offset // 3
        col_start = offset % 3
        window = padded[:, row_start : row_start + side, col_start : col_start + side, :].reshape(
            -1, field.shape[3]
        )
        if field_rows:
            blocks.append(
                lax.dot_general(
                    window, flat_grad, (((0,), (0,)), ((), ())), preferred_element_type=jnp.float32
                )
            )
        else:
            blocks.append(
                lax.dot_general(
                    flat_grad, window, (((0,), (0,)), ((), ())), preferred_element_type=jnp.float32
                )
            )
    stacked = jnp.stack(blocks)
    return stacked.reshape(3, 3, stacked.shape[1], stacked.shape[2])


def action_planes(move, board):
    cells = board * board
    plane = (lax.broadcasted_iota(jnp.int32, (move.shape[0], cells), 1) == move[:, None]).astype(
        jnp.float32
    )
    passed = (move == cells).astype(jnp.float32)
    return (plane.reshape(move.shape[0], board, board, 1), passed[:, None, None, None])


def head_backward(state, head_used, value_now, reward_now, total):
    pooled = jnp.mean(state, axis=(1, 2)).astype(jnp.bfloat16)
    raw = head_scale * jnp.stack(
        [
            jnp.dot(pooled, head_used[0], preferred_element_type=jnp.float32),
            jnp.dot(pooled, head_used[1], preferred_element_type=jnp.float32),
        ]
    )
    squashed = jnp.tanh(raw / soft_cap)
    raised = jnp.exp(soft_cap * squashed)
    chances = raised / jnp.sum(raised, axis=2, keepdims=True)
    targets = jnp.stack([value_now, reward_now])
    picked = (lax.broadcasted_iota(jnp.int32, raw.shape, 2) == targets[:, :, None]).astype(
        jnp.float32
    )
    logit_grad = ((chances - picked) * (1.0 - squashed * squashed) / total).astype(jnp.bfloat16)
    pooled_grad = head_scale * (
        jnp.dot(logit_grad[0], head_used[0].T, preferred_element_type=jnp.float32)
        + jnp.dot(logit_grad[1], head_used[1].T, preferred_element_type=jnp.float32)
    )
    return (pooled, logit_grad, pooled_grad)


def adam_update(param, grad, mean, square):
    mean_new = beta_one * mean + (1.0 - beta_one) * grad
    square_new = beta_two * square + (1.0 - beta_two) * grad * grad
    param_new = param - step_size * mean_new / (jnp.sqrt(square_new) + eps_adam)
    return (param_new, mean_new, square_new)


def local(
    hidden_state,
    actions,
    value_target,
    reward_target,
    kernel_first,
    kernel_second,
    head_weight,
    action_embed,
    first_mean,
    first_square,
    second_mean,
    second_square,
    head_mean,
    head_square,
    embed_mean,
    embed_square,
):
    total = hidden_state.shape[0] * lax.axis_size("dp")
    board = hidden_state.shape[1]
    cells = board * board
    scale = (9.0 * CHANNELS) ** (-0.5)
    first_used, second_used, head_used, embed_used = (
        lax.all_gather(kernel_first.astype(jnp.bfloat16), "dp", axis=2, tiled=True),
        lax.all_gather(kernel_second.astype(jnp.bfloat16), "dp", axis=2, tiled=True),
        lax.all_gather(head_weight.astype(jnp.bfloat16), "dp", axis=1, tiled=True),
        lax.all_gather(action_embed.astype(jnp.bfloat16), "dp", axis=1, tiled=True),
    )
    first_used, second_used, head_used, embed_used = (
        lax.all_gather(first_used, "mp", axis=3, tiled=True),
        lax.all_gather(second_used, "mp", axis=3, tiled=True),
        lax.all_gather(head_used, "mp", axis=0, tiled=True),
        lax.all_gather(embed_used, "mp", axis=0, tiled=True),
    )
    count = hidden_state.shape[0] // lax.axis_size("mp")
    begin = lax.axis_index("mp") * count
    states = lax.dynamic_slice_in_dim(hidden_state, begin, count, 0)
    moves = lax.dynamic_slice_in_dim(actions, begin, count, 0)
    values = lax.dynamic_slice_in_dim(value_target, begin, count, 0)
    rewards = lax.dynamic_slice_in_dim(reward_target, begin, count, 0)
    unroll = moves.shape[1]
    embed = embed_used.astype(jnp.float32)
    state = states.astype(jnp.float32)
    saved = []
    for position in range(unroll):
        plane, passed = action_planes(moves[:, position], board)
        mixed = state + plane * embed[0] + passed * embed[1]
        conv_input = mixed.astype(jnp.bfloat16)
        pre = scale * conv_apply(conv_input, first_used, "HWIO")
        hidden = jax.nn.silu(pre).astype(jnp.bfloat16)
        branch = conv_apply(hidden, second_used, "HWOI")
        summed = mixed + scale * branch
        factor = lax.rsqrt(jnp.mean(summed * summed, axis=(1, 2, 3), keepdims=True) + eps_norm)
        state = summed * factor
        pooled, logit_grad, pooled_grad = head_backward(
            state, head_used, values[:, position], rewards[:, position], total
        )
        saved.append(
            (
                plane,
                passed,
                conv_input,
                pre,
                hidden,
                summed,
                factor,
                pooled,
                logit_grad,
                pooled_grad,
            )
        )
    first_grad = jnp.zeros(first_used.shape, jnp.float32)
    second_grad = jnp.zeros(second_used.shape, jnp.float32)
    head_grad = jnp.zeros(head_used.shape, jnp.float32)
    embed_grad = jnp.zeros(embed_used.shape, jnp.float32)
    carry = jnp.zeros(states.shape, jnp.float32)
    for position in range(unroll - 1, -1, -1):
        plane, passed, conv_input, pre, hidden, summed, factor, pooled, logit_grad, pooled_grad = (
            saved[position]
        )
        state_grad = carry + pooled_grad[:, None, None, :] / cells
        summed_grad = factor * state_grad - factor * factor * factor * summed * jnp.mean(
            state_grad * summed, axis=(1, 2, 3), keepdims=True
        )
        branch_grad = summed_grad.astype(jnp.bfloat16)
        hidden_grad = scale * conv_apply(branch_grad, second_used[::-1, ::-1], "HWIO")
        inner_grad = (hidden_grad * gate_slope(pre)).astype(jnp.bfloat16)
        input_grad = conv_apply(inner_grad, first_used[::-1, ::-1], "HWOI")
        carry = summed_grad + scale * input_grad
        first_grad = first_grad + scale * tap_products(conv_input, inner_grad, True)
        second_grad = second_grad + scale * tap_products(hidden, branch_grad, False)
        head_grad = head_grad + head_scale * jnp.stack(
            [
                lax.dot_general(
                    pooled,
                    logit_grad[0],
                    (((0,), (0,)), ((), ())),
                    preferred_element_type=jnp.float32,
                ),
                lax.dot_general(
                    pooled,
                    logit_grad[1],
                    (((0,), (0,)), ((), ())),
                    preferred_element_type=jnp.float32,
                ),
            ]
        )
        embed_grad = embed_grad + jnp.stack(
            [jnp.sum(plane * carry, axis=(0, 1, 2)), jnp.sum(passed * carry, axis=(0, 1, 2))]
        )
    first_grad, second_grad, head_grad, embed_grad = (
        lax.psum_scatter(first_grad, "mp", scatter_dimension=3, tiled=True),
        lax.psum_scatter(second_grad, "mp", scatter_dimension=3, tiled=True),
        lax.psum_scatter(head_grad, "mp", scatter_dimension=0, tiled=True),
        lax.psum_scatter(embed_grad, "mp", scatter_dimension=0, tiled=True),
    )
    first_grad, second_grad, head_grad, embed_grad = (
        lax.psum_scatter(first_grad, "dp", scatter_dimension=2, tiled=True),
        lax.psum_scatter(second_grad, "dp", scatter_dimension=2, tiled=True),
        lax.psum_scatter(head_grad, "dp", scatter_dimension=1, tiled=True),
        lax.psum_scatter(embed_grad, "dp", scatter_dimension=1, tiled=True),
    )
    first_new, first_mean_new, first_square_new = adam_update(
        kernel_first, first_grad, first_mean, first_square
    )
    second_new, second_mean_new, second_square_new = adam_update(
        kernel_second, second_grad, second_mean, second_square
    )
    head_new, head_mean_new, head_square_new = adam_update(
        head_weight, head_grad, head_mean, head_square
    )
    embed_new, embed_mean_new, embed_square_new = adam_update(
        action_embed, embed_grad, embed_mean, embed_square
    )
    return (
        first_new,
        second_new,
        head_new,
        embed_new,
        first_mean_new,
        first_square_new,
        second_mean_new,
        second_square_new,
        head_mean_new,
        head_square_new,
        embed_mean_new,
        embed_square_new,
        first_grad,
        second_grad,
        head_grad,
        embed_grad,
    )


def solution(mesh):
    placed = (
        P("dp", None, None, None),
        P("dp", None),
        P("dp", None),
        P("dp", None),
        P(None, None, "dp", "mp"),
        P(None, None, "dp", "mp"),
        P("mp", "dp", None),
        P("mp", "dp"),
        P(None, None, "dp", "mp"),
        P(None, None, "dp", "mp"),
        P(None, None, "dp", "mp"),
        P(None, None, "dp", "mp"),
        P("mp", "dp", None),
        P("mp", "dp", None),
        P("mp", "dp"),
        P("mp", "dp"),
    )
    return jax.shard_map(
        local,
        mesh=mesh,
        in_specs=placed,
        out_specs=(
            P(None, None, "dp", "mp"),
            P(None, None, "dp", "mp"),
            P("mp", "dp", None),
            P("mp", "dp"),
            P(None, None, "dp", "mp"),
            P(None, None, "dp", "mp"),
            P(None, None, "dp", "mp"),
            P(None, None, "dp", "mp"),
            P("mp", "dp", None),
            P("mp", "dp", None),
            P("mp", "dp"),
            P("mp", "dp"),
            P(None, None, "dp", "mp"),
            P(None, None, "dp", "mp"),
            P("mp", "dp", None),
            P("mp", "dp"),
        ),
        check_vma=False,
    )
```

profile of v0, /device:TPU:0, one launch (start us, length us, event | category | flops | bytes accessed | tf_op | source)
XLA Modules:
  0.0 581.1 jit_solution(16968905555778703401)
XLA Ops:
  7.3 1.0 convert_element_type.150
  8.3 48.3 %all_gather.26 = bf16[3,3,256,128]{3,2,1,0:T(8,128)(2,1)} all-gather(bf16[3,3,16,128]{3,2,1,0:T(8,128)(2,1)S(1)} %convert_element_type.150), channel_id=1, replica_groups=mesh['dp'=16,'mp'=2] {'dp'}, dimensions={2}, use_global_device_ids=true | all-gather | bytes 626688 | tf_op jit(solution)/shard_map/all_gather | solution.py:121
  56.6 0.9 convert_element_type.152
  57.5 41.0 %all_gather.28 = bf16[3,3,256,128]{3,2,1,0:T(8,128)(2,1)} all-gather(bf16[3,3,16,128]{3,2,1,0:T(8,128)(2,1)S(1)} %convert_element_type.152), channel_id=1, replica_groups=mesh['dp'=16,'mp'=2] {'dp'}, dimensions={2}, use_global_device_ids=true | all-gather | bytes 626688 | tf_op jit(solution)/shard_map/all_gather | solution.py:122
  98.6 0.6 dynamic-slice
  100.1 38.8 %all-reduce.4 = bf16[256]{0:T(256)(128)(2,1)S(1)} all-reduce(bf16[256]{0:T(256)(128)(2,1)S(1)} %dynamic-update-slice), channel_id=1, replica_groups=mesh['dp'=16,'mp'=2] {'dp'}, use_global_device_ids=true, to_apply=%add.4 | all-reduce | flops 256 | bytes 1024
  138.9 1.8 all-gather
  140.8 0.6 fusion.358
  142.6 0.7 fusion.265
  143.7 0.7 fusion.266
  144.4 37.2 %all_gather.30 = bf16[1,256,601]{2,1,0:T(8,128)(2,1)S(1)} all-gather(bf16[1,16,601]{2,1,0:T(8,128)(2,1)S(1)} %convert_element_type.157), channel_id=1, replica_groups=mesh['dp'=16,'mp'=2] {'dp'}, dimensions={1}, use_global_device_ids=true | all-gather | bytes 326944 | tf_op jit(solution)/shard_map/all_gather | solution.py:123
  181.6 0.6 fusion.356
  183.4 1.4 add_reduce_fusion
  184.8 1.4 add_reduce_fusion.1
  186.2 2.4 all_gather.31
  188.6 0.8 fusion.61
  189.5 2.0 fusion.6
  192.3 2.0 convolution_multiply_fusion.3
  194.8 0.8 multiply_reduce_fusion.8
  196.4 0.7 copy-done.1
  197.4 2.1 fusion.5
  199.5 0.8 select_bitcast_fusion.2
  200.4 0.8 convolution_multiply_fusion.2
  201.7 0.8 multiply_reduce_fusion.7
  205.3 0.7 multiply_reduce_fusion.5
  206.8 0.7 fusion.126
  207.8 2.1 fusion.7
  210.6 0.8 convolution_multiply_fusion.1
  211.9 0.8 multiply_reduce_fusion.3
  213.3 0.8 fusion.348
  214.2 1.0 pad.29
  215.3 0.7 slice.243
  216.4 1.2 fusion
  218.3 1.2 fusion.17
  219.6 1.2 fusion.16
  220.8 1.3 fusion.15
  222.1 1.2 fusion.14
  223.4 1.2 fusion.13
  224.6 1.2 fusion.12
  225.9 1.2 fusion.11
  227.1 1.3 fusion.10
  228.4 1.2 fusion.9
  229.8 0.9 reshape.830
  230.6 1.0 slice_bitcast_fusion.9
  231.6 1.2 fusion.26
  235.6 2.0 add_multiply_fusion
  237.7 0.8 copy-done.8
  238.7 2.0 fusion.8
  247.1 1.7 add_multiply_fusion.1
  250.2 0.8 convolution_multiply_fusion
  251.8 2.5 all-reduce.5
  254.2 0.7 constant_dynamic-slice_fusion.4
  254.9 0.8 copy.106
  255.8 0.7 reduce-scatter.20.cloned.1.call-update
  256.5 0.7 reduce-scatter.16.cloned.1.call-update
  257.3 1.5 reduce-scatter.10.cloned.1.call-done
  258.8 80.4 %reduce-scatter.22.cloned.1.call-done = f32[16,1]{1,0:T(8,128)} async-done(((f32[256,1]{1,0:T(8,128)}), f32[16,1]{1,0:T(8,128)}) %reduce-scatter.22.cloned.1.call-update) | async-done | bytes 80
  339.2 0.8 copy.107
  340.5 75.6 %reduce-scatter.20.cloned.1.call-done = f32[1,16,601]{2,1,0:T(8,128)} async-done(((f32[1,256,601]{2,1,0:T(8,128)}), f32[1,16,601]{2,1,0:T(8,128)}) %reduce-scatter.20.cloned.1.call-update) | async-done | bytes 38480 | tf_op jit(solution)/shard_map/reduce_scatter | solution.py:217
  416.1 1.4 divide_subtract_fusion.2
  417.6 77.1 %reduce-scatter.16.cloned.1.call-done = f32[3,3,16,128]{3,2,1,0:T(8,128)} async-done(((f32[3,3,256,128]{3,2,1,0:T(8,128)}), f32[3,3,16,128]{3,2,1,0:T(8,128)}) %reduce-scatter.16.cloned.1.call-update) | async-done | bytes 73744 | tf_op jit(solution)/shard_map/reduce_scatter | solution.py:216
  494.6 1.6 divide_subtract_fusion
  496.2 76.8 %reduce-scatter.12.cloned.1.call-done = f32[3,3,16,128]{3,2,1,0:T(8,128)} async-done(((f32[3,3,256,128]{3,2,1,0:T(8,128)}), f32[3,3,16,128]{3,2,1,0:T(8,128)}) %reduce-scatter.12.cloned.1.call-update) | async-done | bytes 73744 | tf_op jit(solution)/shard_map/reduce_scatter | solution.py:215
  573.0 1.6 divide_subtract_fusion.1
  (206 shorter events, 20.9 us)
Async XLA Ops:
  7.2 136.1 %copy-start = (bf16[2,19,19,256]{3,0,2,1:T(2,128)(2,1)S(1)}, bf16[2,19,19,256]{3,0,2,1:T(2,128)(2,1)}, u32[]{:S(2)}) copy-start(bf16[2,19,19,256]{3,0,2,1:T(2,128)(2,1)} %param.16) | copy-start | bytes 1108996
  7.2 91.4 %copy-start.38 = (u32[32]{0:T(128)S(1)}, u32[32]{0:T(128)}, u32[]{:S(2)}) copy-start(u32[32]{0:T(128)} %constant.145) | copy-start | bytes 388
  7.2 91.4 %copy-start.28 = (f32[1,16]{1,0:T(1,128)S(1)}, f32[1,16]{1,0:T(1,128)}, u32[]{:S(2)}) copy-start(f32[1,16]{1,0:T(1,128)} %param.23) | copy-start | bytes 196
  7.2 133.5 %copy-start.36 = (s32[2,2]{1,0:T(2,128)S(1)}, s32[2,2]{1,0:T(2,128)}, u32[]{:S(2)}) copy-start(s32[2,2]{1,0:T(2,128)} %param.17) | copy-start | bytes 52
  7.2 137.1 %copy-start.17 = (f32[1,16,601]{2,1,0:T(8,128)S(1)}, f32[1,16,601]{2,1,0:T(8,128)}, u32[]{:S(2)}) copy-start(f32[1,16,601]{2,1,0:T(8,128)} %param.22) | copy-start | bytes 115396
  7.2 174.4 %copy-start.32 = (s32[2,2]{1,0:T(2,128)S(1)}, s32[2,2]{1,0:T(2,128)}, u32[]{:S(2)}) copy-start(s32[2,2]{1,0:T(2,128)} %param.18) | copy-start | bytes 52
  7.3 174.4 %copy-start.31 = (s32[2,2]{1,0:T(2,128)S(1)}, s32[2,2]{1,0:T(2,128)}, u32[]{:S(2)}) copy-start(s32[2,2]{1,0:T(2,128)} %param.19) | copy-start | bytes 52
  7.3 182.2 %all-gather.4.cloned.1.call-start = ((), (), s32[]{:S(2)}) async-start(), calls=%async_computation.7 | async-start | bytes 1769472 | tf_op jit(solution)/shard_map/all_gather | solution.py:127
  56.6 135.1 %all-gather.6.cloned.1.call-start = ((), (), s32[]{:S(2)}) async-start(), calls=%async_computation.8 | async-start | bytes 1769472 | tf_op jit(solution)/shard_map/all_gather | solution.py:128
  98.5 157.2 %reduce-scatter.18.cloned.1.call-start = ((), (), s32[]{:S(2)}) async-start(), calls=%async_computation.13 | async-start | bytes 1966080 | tf_op jit(solution)/shard_map/reduce_scatter | solution.py:211
  181.6 7.9 %copy-start.26 = (pred[8,3]{0,1:T(4,128)(4,1)S(1)}, pred[8,3]{0,1:T(4,128)(4,1)}, u32[]{:S(2)}) copy-start(pred[8,3]{0,1:T(4,128)(4,1)} %constant.135) | copy-start | bytes 76
  191.5 0.8 copy-start.9
  196.4 0.7 copy-start.1
  197.4 3.0 copy-start.35
  199.5 0.9 copy-start.11
  204.5 3.3 copy-start.12
  207.8 2.8 copy-start.33
  209.9 0.7 copy-start.5
  215.3 2.3 copy-start.7
  217.7 38.8 %reduce-scatter.14.cloned.1.call-start = ((), (), s32[]{:S(2)}) async-start(), calls=%async_computation.11 | async-start | bytes 3538944 | tf_op jit(solution)/shard_map/reduce_scatter | solution.py:210
  227.1 2.5 copy-start.3
  230.6 2.2 copy-start.16
  233.2 0.9 copy-start.4
  237.6 0.9 copy-start.8
  237.6 1.1 copy-start.10
  237.6 1.2 copy-start.19
  237.6 3.1 copy-start.6
  237.6 3.8 copy-start.15
  237.6 21.2 %reduce-scatter.10.cloned.1.call-start = ((), (), s32[]{:S(2)}) async-start(), calls=%async_computation.9 | async-start | bytes 3538944 | tf_op jit(solution)/shard_map/reduce_scatter | solution.py:209
  243.5 1.0 copy-start.2
  248.8 0.7 copy-start.37
  248.8 1.4 copy-start.34
  248.9 90.3 %reduce-scatter.22.cloned.1.call-start = ((), (), s32[]{:S(2)}) async-start(), calls=%async_computation.15 | async-start | bytes 139264
  251.5 88.5 %copy-start.29 = (f32[1,16]{1,0:T(1,128)S(1)}, f32[1,16]{1,0:T(1,128)}, u32[]{:S(2)}) copy-start(f32[1,16]{1,0:T(1,128)} %param.30) | copy-start | bytes 196
  251.5 88.5 %copy-start.30 = (f32[1,16]{1,0:T(1,128)S(1)}, f32[1,16]{1,0:T(1,128)}, u32[]{:S(2)}) copy-start(f32[1,16]{1,0:T(1,128)} %param.31) | copy-start | bytes 196
  251.5 164.7 %copy-start.18 = (f32[1,16,601]{2,1,0:T(8,128)S(1)}, f32[1,16,601]{2,1,0:T(8,128)}, u32[]{:S(2)}) copy-start(f32[1,16,601]{2,1,0:T(8,128)} %param.22) | copy-start | bytes 115396
  251.5 164.6 %copy-start.24 = (f32[1,16,601]{2,1,0:T(8,128)S(1)}, f32[1,16,601]{2,1,0:T(8,128)}, u32[]{:S(2)}) copy-start(f32[1,16,601]{2,1,0:T(8,128)} %param.28) | copy-start | bytes 115396
  251.5 164.6 %copy-start.25 = (f32[1,16,601]{2,1,0:T(8,128)S(1)}, f32[1,16,601]{2,1,0:T(8,128)}, u32[]{:S(2)}) copy-start(f32[1,16,601]{2,1,0:T(8,128)} %param.29) | copy-start | bytes 115396
  251.5 243.1 %copy-start.13 = (f32[3,3,16,128]{3,2,1,0:T(8,128)S(1)}, f32[3,3,16,128]{3,2,1,0:T(8,128)}, u32[]{:S(2)}) copy-start(f32[3,3,16,128]{3,2,1,0:T(8,128)} %param.21) | copy-start | bytes 221188
  251.5 243.1 %copy-start.20 = (f32[3,3,16,128]{3,2,1,0:T(8,128)S(1)}, f32[3,3,16,128]{3,2,1,0:T(8,128)}, u32[]{:S(2)}) copy-start(f32[3,3,16,128]{3,2,1,0:T(8,128)} %param.26) | copy-start | bytes 221188
  251.5 243.1 %copy-start.21 = (f32[3,3,16,128]{3,2,1,0:T(8,128)S(1)}, f32[3,3,16,128]{3,2,1,0:T(8,128)}, u32[]{:S(2)}) copy-start(f32[3,3,16,128]{3,2,1,0:T(8,128)} %param.27) | copy-start | bytes 221188
  251.5 321.5 %copy-start.14 = (f32[3,3,16,128]{3,2,1,0:T(8,128)S(1)}, f32[3,3,16,128]{3,2,1,0:T(8,128)}, u32[]{:S(2)}) copy-start(f32[3,3,16,128]{3,2,1,0:T(8,128)} %param.20) | copy-start | bytes 221188
  251.6 321.5 %copy-start.22 = (f32[3,3,16,128]{3,2,1,0:T(8,128)S(1)}, f32[3,3,16,128]{3,2,1,0:T(8,128)}, u32[]{:S(2)}) copy-start(f32[3,3,16,128]{3,2,1,0:T(8,128)} %param.24) | copy-start | bytes 221188
  251.6 321.4 %copy-start.23 = (f32[3,3,16,128]{3,2,1,0:T(8,128)S(1)}, f32[3,3,16,128]{3,2,1,0:T(8,128)}, u32[]{:S(2)}) copy-start(f32[3,3,16,128]{3,2,1,0:T(8,128)} %param.25) | copy-start | bytes 221188
  255.7 160.4 %reduce-scatter.20.cloned.1.call-start = ((), (), s32[]{:S(2)}) async-start(), calls=%async_computation.14 | async-start | bytes 696320 | tf_op jit(solution)/shard_map/reduce_scatter | solution.py:217
  256.5 238.2 %reduce-scatter.16.cloned.1.call-start = ((), (), s32[]{:S(2)}) async-start(), calls=%async_computation.12 | async-start | bytes 1253376 | tf_op jit(solution)/shard_map/reduce_scatter | solution.py:216
  257.2 315.8 %reduce-scatter.12.cloned.1.call-start = ((), (), s32[]{:S(2)}) async-start(), calls=%async_computation.10 | async-start | bytes 1253376 | tf_op jit(solution)/shard_map/reduce_scatter | solution.py:215
  340.0 234.7 %copy-start.27 = (f32[1,16]{1,0:T(1,128)}, f32[1,16]{1,0:T(1,128)S(1)}, u32[]{:S(2)}) copy-start(f32[1,16]{1,0:T(1,128)S(1)} %copy.107) | copy-start | bytes 196
Sparse Core Ops, SparseCore 0:
  56.7 4.7 all-gather.3
  98.7 6.9 all-gather.5
  217.8 6.4 reduce-scatter.17
  237.7 7.6 reduce-scatter.13
  249.0 9.7 reduce-scatter.9
  260.9 78.2 reduce-scatter.21
  342.0 74.0 reduce-scatter.19
  419.0 75.6 reduce-scatter.15
  497.5 75.4 reduce-scatter.11
where the time goes:
time: 582 us; the launch traced here: 581 us
  waiting for transfers between devices  313 us (54%)
  blocking collectives  172 us (30%)
  matrix products  33.7 us (6%)
  other arithmetic  24.3 us (4%)
  between operations  19.6 us (3%)
  local copies, waits for them, and re-layouts  18.2 us (3%)
    unnamed x10, waiting for transfers between devices  81.8 us
    reduce_scatter x1, waiting for transfers between devices, local(): lax.psum_scatter(second_grad, 'dp', scatter_dimension=2, tiled=True)  77.1 us
    reduce_scatter x1, waiting for transfers between devices, local(): lax.psum_scatter(first_grad, 'dp', scatter_dimension=2, tiled=True)  76.8 us
    reduce_scatter x1, waiting for transfers between devices, local(): lax.psum_scatter(head_grad, 'dp', scatter_dimension=1, tiled=True)  75.6 us
    all_gather x1, blocking collectives, local(): lax.all_gather(kernel_first.astype(jnp.bfloat16), 'dp', axis=2, tiled=True)  48.3 us
    unnamed x2, blocking collectives  41.3 us
    all_gather x1, blocking collectives, local(): lax.all_gather(kernel_second.astype(jnp.bfloat16), 'dp', axis=2, tiled=True)  41 us
    all_gather x1, blocking collectives, local(): lax.all_gather(head_weight.astype(jnp.bfloat16), 'dp', axis=1, tiled=True)  37.2 us
  transfers between devices with their start and end apart: 9, of which 5 were waited for; matrix products, arithmetic and copies ran while one was open for 8% of the time, Pallas kernels for 0%

commit v1 on v0

--- a/solution.py
+++ b/solution.py
@@ -11,6 +11,19 @@
 beta_two = 0.999
 step_size = 0.1
 eps_adam = 1e-08
+
+
+def ring_gather(array, axis, dim):
+    ways = lax.axis_size(axis)
+    up = [(d, (d + 1) % ways) for d in range(ways)]
+    down = [(d, (d - 1) % ways) for d in range(ways)]
+    earlier, later = ([array], [array])
+    for _ in range(ways // 2):
+        earlier.append(lax.ppermute(earlier[-1], axis, up))
+    for _ in range((ways - 1) // 2):
+        later.append(lax.ppermute(later[-1], axis, down))
+    line = jnp.concatenate([*earlier[::-1], *later[1:]], axis=dim)
+    return jnp.roll(line, (lax.axis_index(axis) - ways // 2) * array.shape[dim], axis=dim)
 
 
 def conv_apply(field, kernel, layout):
@@ -120,7 +133,7 @@
     first_used, second_used, head_used, embed_used = (
         lax.all_gather(kernel_first.astype(jnp.bfloat16), "dp", axis=2, tiled=True),
         lax.all_gather(kernel_second.astype(jnp.bfloat16), "dp", axis=2, tiled=True),
-        lax.all_gather(head_weight.astype(jnp.bfloat16), "dp", axis=1, tiled=True),
+        ring_gather(head_weight.astype(jnp.bfloat16), "dp", 1),
         lax.all_gather(action_embed.astype(jnp.bfloat16), "dp", axis=1, tiled=True),
     )
     first_used, second_used, head_used, embed_used = (

time: 582 us -> 615 us (1.057)
  starting transfers between devices: 0.59 us -> 41.6 us
  blocking collectives: 172 us -> 135 us
  waiting for transfers between devices: 313 us -> 333 us
  local copies, waits for them, and re-layouts: 18.2 us -> 27.4 us
    ppermute x0 -> x15, starting transfers between devices: none -> 41 us  [the longest x7 40.4 us: ring_gather(): later.append(lax.ppermute(later[-1], axis, down))]
    all_gather x1 -> x0, blocking collectives: 37.2 us -> none  [local(): lax.all_gather(head_weight.astype(jnp.bfloat16), 'dp', axis=1, tiled=True)]
    ppermute x0 -> x15, waiting for transfers between devices: none -> 21.5 us  [the longest x8 20.9 us: ring_gather(): earlier.append(lax.ppermute(earlier[-1], axis, up))]
    concatenate x0 -> x1, local copies, waits for them, and re-layouts: none -> 7.64 us  [ring_gather(): jnp.roll(line, (lax.axis_index(axis) - ways // 2) * array.shape[dim], axi...]
  transfers between devices with their start and end apart: 9 -> 24, of which waited for: 5 -> 14; matrix products, arithmetic and copies ran while one was open for 8% -> 9% of each run, Pallas kernels for 0% -> 0%
where the time goes in v1:
time: 615 us; the launch traced here: 614 us
  waiting for transfers between devices  333 us (54%)
  blocking collectives  135 us (22%)
  starting transfers between devices  41.6 us (7%)
  matrix products  33.8 us (5%)
  local copies, waits for them, and re-layouts  27.4 us (4%)
  other arithmetic  24.2 us (4%)
  between operations  19.7 us (3%)
    unnamed x10, waiting for transfers between devices  81.6 us
    reduce_scatter x1, waiting for transfers between devices, local(): lax.psum_scatter(first_grad, 'dp', scatter_dimension=2, tiled=True)  76.9 us
    reduce_scatter x1, waiting for transfers between devices, local(): lax.psum_scatter(second_grad, 'dp', scatter_dimension=2, tiled=True)  76.7 us
    reduce_scatter x1, waiting for transfers between devices, local(): lax.psum_scatter(head_grad, 'dp', scatter_dimension=1, tiled=True)  75.7 us
    all_gather x1, blocking collectives, local(): lax.all_gather(kernel_first.astype(jnp.bfloat16), 'dp', axis=2, tiled=True)  48.4 us
    all_gather x1, blocking collectives, local(): lax.all_gather(kernel_second.astype(jnp.bfloat16), 'dp', axis=2, tiled=True)  41.5 us
    unnamed x2, blocking collectives  40.6 us
    ppermute x7, starting transfers between devices, ring_gather(): later.append(lax.ppermute(later[-1], axis, down))  40.4 us
  transfers between devices with their start and end apart: 24, of which 14 were waited for; matrix products, arithmetic and copies ran while one was open for 9% of the time, Pallas kernels for 0%

profile of v1, /device:TPU:0, one launch (start us, length us, event | category | flops | bytes accessed | tf_op | source)
XLA Modules:
  0.0 614.1 jit_solution(11987569932995698358)
XLA Ops:
  7.3 0.9 convert_element_type.150
  8.2 48.4 %all_gather.23 = bf16[3,3,256,128]{3,2,1,0:T(8,128)(2,1)} all-gather(bf16[3,3,16,128]{3,2,1,0:T(8,128)(2,1)S(1)} %convert_element_type.150), channel_id=1, replica_groups=mesh['dp'=16,'mp'=2] {'dp'}, dimensions={2}, use_global_device_ids=true | all-gather | bytes 626688 | tf_op jit(solution)/shard_map/all_gather | solution.py:134
  56.7 0.9 copy.77
  57.7 5.6 collective-permute-start.8
  63.3 0.9 convert_element_type.152
  64.2 41.5 %all_gather.25 = bf16[3,3,256,128]{3,2,1,0:T(8,128)(2,1)} all-gather(bf16[3,3,16,128]{3,2,1,0:T(8,128)(2,1)S(1)} %convert_element_type.152), channel_id=1, replica_groups=mesh['dp'=16,'mp'=2] {'dp'}, dimensions={2}, use_global_device_ids=true | all-gather | bytes 626688 | tf_op jit(solution)/shard_map/all_gather | solution.py:135
  109.3 38.1 %all-reduce.4 = bf16[256]{0:T(256)(128)(2,1)S(1)} all-reduce(bf16[256]{0:T(256)(128)(2,1)S(1)} %dynamic-update-slice), channel_id=1, replica_groups=mesh['dp'=16,'mp'=2] {'dp'}, use_global_device_ids=true, to_apply=%add.4 | all-reduce | flops 256 | bytes 1024
  147.4 1.8 all-gather
  150.9 5.2 collective-permute-start.9
  156.2 4.0 collective-permute-done.1
  160.1 0.8 fusion.61
  161.0 5.6 collective-permute-start.10
  166.6 2.4 collective-permute-done.2
  169.7 5.9 collective-permute-start.11
  175.5 2.4 collective-permute-done.3
  178.3 6.1 collective-permute-start.12
  184.4 2.4 collective-permute-done.4
  187.4 5.8 collective-permute-start.13
  193.2 2.4 collective-permute-done.5
  196.0 6.2 %collective-permute-start.14 = (bf16[1,16,601]{1,2,0:T(8,128)(2,1)}, bf16[1,16,601]{1,2,0:T(8,128)(2,1)}, u32[]{:S(2)}, u32[]{:S(2)}) collective-permute-start(bf16[1,16,601]{1,2,0:T(8,128)(2,1)} %collective-permute-done.13), channel_id=1, source_target_pairs={{0,30},{2,0},{4,2},{6,4},{8,6},{10,8},{12,10},{14,12},{16,14},{18,... | collective-permute-start | bytes 57704 | tf_op jit(solution)/shard_map/ppermute | solution.py:24
  202.2 2.4 collective-permute-done.6
  206.1 2.7 add_reduce_fusion
  208.9 4.9 collective-permute-done.7
  213.7 7.6 %concatenate.30 = bf16[1,512,601]{1,2,0:T(8,128)(2,1)S(1)} concatenate(bf16[1,16,601]{1,2,0:T(8,128)(2,1)} %collective-permute-done.7, bf16[1,16,601]{1,2,0:T(8,128)(2,1)} %collective-permute-done.6, bf16[1,16,601]{1,2,0:T(8,128)(2,1)} %copy-done.9, bf16[1,16,601]{1,2,0:T(8,128)(2,1)S(1)} %collective-permute-done.4, bf16[1,16,601]{1,2,0:T(8,128)(2,1)S(1)} %collective-permute-done.3, ...), dimensions={1} | concatenate | bytes 1230848 | tf_op jit(solution)/shard_map/jit(_roll_dynamic)/concatenate | solution.py:26
  221.6 2.4 all_gather.27
  224.0 2.1 fusion.6
  226.9 2.0 convolution_multiply_fusion.3
  229.4 0.8 multiply_reduce_fusion.8
  232.0 2.1 fusion.5
  234.1 0.9 select_bitcast_fusion.2
  236.3 0.8 multiply_reduce_fusion.7
  242.5 2.1 fusion.7
  245.3 0.8 convolution_multiply_fusion.1
  246.5 0.8 multiply_reduce_fusion.3
  248.0 0.8 fusion.348
  248.8 1.0 pad.29
  251.1 1.2 fusion
  253.0 1.2 fusion.17
  254.2 1.3 fusion.16
  255.6 1.2 fusion.15
  256.8 1.2 fusion.14
  258.1 1.2 fusion.13
  259.3 1.2 fusion.12
  260.5 1.2 fusion.11
  261.8 1.3 fusion.10
  263.0 1.2 fusion.9
  264.4 0.9 reshape.830
  265.3 1.0 slice_bitcast_fusion.9
  266.3 1.2 fusion.26
  270.3 2.0 add_multiply_fusion
  272.4 0.8 copy-done.8
  273.4 2.0 fusion.8
  281.8 1.8 add_multiply_fusion.1
  284.9 0.8 convolution_multiply_fusion
  286.5 2.5 all-reduce.5
  289.6 0.8 copy.88
  292.7 79.7 %reduce-scatter.22.cloned.1.call-done = f32[16,1]{1,0:T(8,128)} async-done(((f32[256,1]{1,0:T(8,128)}), f32[16,1]{1,0:T(8,128)}) %reduce-scatter.22.cloned.1.call-update) | async-done | bytes 80
  372.4 0.8 copy.89
  373.7 75.7 %reduce-scatter.20.cloned.1.call-done = f32[1,16,601]{2,1,0:T(8,128)} async-done(((f32[1,256,601]{2,1,0:T(8,128)}), f32[1,16,601]{2,1,0:T(8,128)}) %reduce-scatter.20.cloned.1.call-update) | async-done | bytes 38480 | tf_op jit(solution)/shard_map/reduce_scatter | solution.py:230
  449.4 1.4 divide_subtract_fusion.2
  450.9 76.7 %reduce-scatter.16.cloned.1.call-done = f32[3,3,16,128]{3,2,1,0:T(8,128)} async-done(((f32[3,3,256,128]{3,2,1,0:T(8,128)}), f32[3,3,16,128]{3,2,1,0:T(8,128)}) %reduce-scatter.16.cloned.1.call-update) | async-done | bytes 73744 | tf_op jit(solution)/shard_map/reduce_scatter | solution.py:229
  527.5 1.6 divide_subtract_fusion
  529.1 76.9 %reduce-scatter.12.cloned.1.call-done = f32[3,3,16,128]{3,2,1,0:T(8,128)} async-done(((f32[3,3,256,128]{3,2,1,0:T(8,128)}), f32[3,3,16,128]{3,2,1,0:T(8,128)}) %reduce-scatter.12.cloned.1.call-update) | async-done | bytes 73744 | tf_op jit(solution)/shard_map/reduce_scatter | solution.py:228
  606.0 1.6 divide_subtract_fusion.1
  (236 shorter events, 32.1 us)
Async XLA Ops:
  7.2 142.0 %copy-start = (bf16[2,19,19,256]{3,0,2,1:T(2,128)(2,1)S(1)}, bf16[2,19,19,256]{3,0,2,1:T(2,128)(2,1)}, u32[]{:S(2)}) copy-start(bf16[2,19,19,256]{3,0,2,1:T(2,128)(2,1)} %param.16) | copy-start | bytes 1108996
  7.2 100.6 %copy-start.38 = (u32[32]{0:T(128)S(1)}, u32[32]{0:T(128)}, u32[]{:S(2)}) copy-start(u32[32]{0:T(128)} %constant.175) | copy-start | bytes 388
  7.2 98.6 %copy-start.34 = (s32[2,2]{1,0:T(2,128)S(1)}, s32[2,2]{1,0:T(2,128)}, u32[]{:S(2)}) copy-start(s32[2,2]{1,0:T(2,128)} %param.17) | copy-start | bytes 52
  7.2 100.5 %copy-start.28 = (f32[1,16]{1,0:T(1,128)S(1)}, f32[1,16]{1,0:T(1,128)}, u32[]{:S(2)}) copy-start(f32[1,16]{1,0:T(1,128)} %param.23) | copy-start | bytes 196
  7.2 216.8 %all-gather.4.cloned.1.call-start = ((), (), s32[]{:S(2)}) async-start(), calls=%async_computation.7 | async-start | bytes 1769472 | tf_op jit(solution)/shard_map/all_gather | solution.py:140
  8.2 169.7 %copy-start.35 = (s32[2,2]{1,0:T(2,128)S(1)}, s32[2,2]{1,0:T(2,128)}, u32[]{:S(2)}) copy-start(s32[2,2]{1,0:T(2,128)} %param.18) | copy-start | bytes 52
  8.2 187.5 %copy-start.36 = (s32[2,2]{1,0:T(2,128)S(1)}, s32[2,2]{1,0:T(2,128)}, u32[]{:S(2)}) copy-start(s32[2,2]{1,0:T(2,128)} %param.19) | copy-start | bytes 52
  56.7 169.7 %all-gather.6.cloned.1.call-start = ((), (), s32[]{:S(2)}) async-start(), calls=%async_computation.8 | async-start | bytes 1769472 | tf_op jit(solution)/shard_map/all_gather | solution.py:141
  57.7 92.6 %collective-permute-start = (bf16[1,16,601]{1,2,0:T(8,128)(2,1)S(1)}, bf16[1,16,601]{1,2,0:T(8,128)(2,1)S(1)}, u32[]{:S(2)}, u32[]{:S(2)}) collective-permute-start(bf16[1,16,601]{1,2,0:T(8,128)(2,1)S(1)} %copy.77), channel_id=1, source_target_pairs={{0,2},{2,4},{4,6},{6,8},{8,10},{10,12},{12,14},{14,16},{16,18},{18... | collective-permute-start | bytes 57704 | tf_op jit(solution)/shard_map/ppermute | solution.py:22
  57.7 93.2 %collective-permute-start.8 = (bf16[1,16,601]{1,2,0:T(8,128)(2,1)S(1)}, bf16[1,16,601]{1,2,0:T(8,128)(2,1)S(1)}, u32[]{:S(2)}, u32[]{:S(2)}) collective-permute-start(bf16[1,16,601]{1,2,0:T(8,128)(2,1)S(1)} %copy.77), channel_id=1, source_target_pairs={{0,30},{2,0},{4,2},{6,4},{8,6},{10,8},{12,10},{14,12},{16,14},{18,... | collective-permute-start | bytes 57704 | tf_op jit(solution)/shard_map/ppermute | solution.py:24
  105.8 184.8 %reduce-scatter.18.cloned.1.call-start = ((), (), s32[]{:S(2)}) async-start(), calls=%async_computation.13 | async-start | bytes 1966080 | tf_op jit(solution)/shard_map/reduce_scatter | solution.py:224
  150.3 9.8 %collective-permute-start.1 = (bf16[1,16,601]{1,2,0:T(8,128)(2,1)S(1)}, bf16[1,16,601]{1,2,0:T(8,128)(2,1)S(1)}, u32[]{:S(2)}, u32[]{:S(2)}) collective-permute-start(bf16[1,16,601]{1,2,0:T(8,128)(2,1)S(1)} %collective-permute-done), channel_id=1, source_target_pairs={{0,2},{2,4},{4,6},{6,8},{8,10},{10,12},{12,14},{14,16},{16,18},{18... | collective-permute-start | bytes 57704 | tf_op jit(solution)/shard_map/ppermute | solution.py:22
  150.9 10.0 %collective-permute-start.9 = (bf16[1,16,601]{1,2,0:T(8,128)(2,1)S(1)}, bf16[1,16,601]{1,2,0:T(8,128)(2,1)S(1)}, u32[]{:S(2)}, u32[]{:S(2)}) collective-permute-start(bf16[1,16,601]{1,2,0:T(8,128)(2,1)S(1)} %collective-permute-done.8), channel_id=1, source_target_pairs={{0,30},{2,0},{4,2},{6,4},{8,6},{10,8},{12,10},{14,12},{16,14},{18,... | collective-permute-start | bytes 57704 | tf_op jit(solution)/shard_map/ppermute | solution.py:24
  160.1 8.8 %collective-permute-start.2 = (bf16[1,16,601]{1,2,0:T(8,128)(2,1)S(1)}, bf16[1,16,601]{1,2,0:T(8,128)(2,1)S(1)}, u32[]{:S(2)}, u32[]{:S(2)}) collective-permute-start(bf16[1,16,601]{1,2,0:T(8,128)(2,1)S(1)} %collective-permute-done.1), channel_id=1, source_target_pairs={{0,2},{2,4},{4,6},{6,8},{8,10},{10,12},{12,14},{14,16},{16,18},{18... | collective-permute-start | bytes 57704 | tf_op jit(solution)/shard_map/ppermute | solution.py:22
  161.0 8.7 %collective-permute-start.10 = (bf16[1,16,601]{1,2,0:T(8,128)(2,1)S(1)}, bf16[1,16,601]{1,2,0:T(8,128)(2,1)S(1)}, u32[]{:S(2)}, u32[]{:S(2)}) collective-permute-start(bf16[1,16,601]{1,2,0:T(8,128)(2,1)S(1)} %collective-permute-done.9), channel_id=1, source_target_pairs={{0,30},{2,0},{4,2},{6,4},{8,6},{10,8},{12,10},{14,12},{16,14},{18,... | collective-permute-start | bytes 57704 | tf_op jit(solution)/shard_map/ppermute | solution.py:24
  169.0 8.9 %collective-permute-start.3 = (bf16[1,16,601]{1,2,0:T(8,128)(2,1)S(1)}, bf16[1,16,601]{1,2,0:T(8,128)(2,1)S(1)}, u32[]{:S(2)}, u32[]{:S(2)}) collective-permute-start(bf16[1,16,601]{1,2,0:T(8,128)(2,1)S(1)} %collective-permute-done.2), channel_id=1, source_target_pairs={{0,2},{2,4},{4,6},{6,8},{8,10},{10,12},{12,14},{14,16},{16,18},{18... | collective-permute-start | bytes 57704 | tf_op jit(solution)/shard_map/ppermute | solution.py:22
  169.7 8.6 %collective-permute-start.11 = (bf16[1,16,601]{1,2,0:T(8,128)(2,1)S(1)}, bf16[1,16,601]{1,2,0:T(8,128)(2,1)S(1)}, u32[]{:S(2)}, u32[]{:S(2)}) collective-permute-start(bf16[1,16,601]{1,2,0:T(8,128)(2,1)S(1)} %collective-permute-done.10), channel_id=1, source_target_pairs={{0,30},{2,0},{4,2},{6,4},{8,6},{10,8},{12,10},{14,12},{16,14},{18,... | collective-permute-start | bytes 57704 | tf_op jit(solution)/shard_map/ppermute | solution.py:24
  177.9 8.9 %collective-permute-start.4 = (bf16[1,16,601]{1,2,0:T(8,128)(2,1)S(1)}, bf16[1,16,601]{1,2,0:T(8,128)(2,1)S(1)}, u32[]{:S(2)}, u32[]{:S(2)}) collective-permute-start(bf16[1,16,601]{1,2,0:T(8,128)(2,1)S(1)} %collective-permute-done.3), channel_id=1, source_target_pairs={{0,2},{2,4},{4,6},{6,8},{8,10},{10,12},{12,14},{14,16},{16,18},{18... | collective-permute-start | bytes 57704 | tf_op jit(solution)/shard_map/ppermute | solution.py:22
  178.3 9.1 %collective-permute-start.12 = (bf16[1,16,601]{1,2,0:T(8,128)(2,1)S(1)}, bf16[1,16,601]{1,2,0:T(8,128)(2,1)S(1)}, u32[]{:S(2)}, u32[]{:S(2)}) collective-permute-start(bf16[1,16,601]{1,2,0:T(8,128)(2,1)S(1)} %collective-permute-done.11), channel_id=1, source_target_pairs={{0,30},{2,0},{4,2},{6,4},{8,6},{10,8},{12,10},{14,12},{16,14},{18,... | collective-permute-start | bytes 57704 | tf_op jit(solution)/shard_map/ppermute | solution.py:24
  186.8 8.8 %collective-permute-start.5 = (bf16[1,16,601]{1,2,0:T(8,128)(2,1)S(1)}, bf16[1,16,601]{1,2,0:T(8,128)(2,1)S(1)}, u32[]{:S(2)}, u32[]{:S(2)}) collective-permute-start(bf16[1,16,601]{1,2,0:T(8,128)(2,1)S(1)} %collective-permute-done.4), channel_id=1, source_target_pairs={{0,2},{2,4},{4,6},{6,8},{8,10},{10,12},{12,14},{14,16},{16,18},{18... | collective-permute-start | bytes 57704 | tf_op jit(solution)/shard_map/ppermute | solution.py:22
  187.4 8.6 %collective-permute-start.13 = (bf16[1,16,601]{1,2,0:T(8,128)(2,1)S(1)}, bf16[1,16,601]{1,2,0:T(8,128)(2,1)}, u32[]{:S(2)}, u32[]{:S(2)}) collective-permute-start(bf16[1,16,601]{1,2,0:T(8,128)(2,1)S(1)} %collective-permute-done.12), channel_id=1, source_target_pairs={{0,30},{2,0},{4,2},{6,4},{8,6},{10,8},{12,10},{14,12},{16,14},{18,... | collective-permute-start | bytes 57704 | tf_op jit(solution)/shard_map/ppermute | solution.py:24
  195.7 9.6 %copy-start.9 = (bf16[1,16,601]{1,2,0:T(8,128)(2,1)}, bf16[1,16,601]{1,2,0:T(8,128)(2,1)S(1)}, u32[]{:S(2)}) copy-start(bf16[1,16,601]{1,2,0:T(8,128)(2,1)S(1)} %collective-permute-done.5) | copy-start | bytes 57700
  195.7 8.9 %collective-permute-start.6 = (bf16[1,16,601]{1,2,0:T(8,128)(2,1)S(1)}, bf16[1,16,601]{1,2,0:T(8,128)(2,1)}, u32[]{:S(2)}, u32[]{:S(2)}) collective-permute-start(bf16[1,16,601]{1,2,0:T(8,128)(2,1)S(1)} %collective-permute-done.5), channel_id=1, source_target_pairs={{0,2},{2,4},{4,6},{6,8},{8,10},{10,12},{12,14},{14,16},{16,18},{18... | collective-permute-start | bytes 57704 | tf_op jit(solution)/shard_map/ppermute | solution.py:22
  196.0 12.9 %collective-permute-start.14 = (bf16[1,16,601]{1,2,0:T(8,128)(2,1)}, bf16[1,16,601]{1,2,0:T(8,128)(2,1)}, u32[]{:S(2)}, u32[]{:S(2)}) collective-permute-start(bf16[1,16,601]{1,2,0:T(8,128)(2,1)} %collective-permute-done.13), channel_id=1, source_target_pairs={{0,30},{2,0},{4,2},{6,4},{8,6},{10,8},{12,10},{14,12},{16,14},{18,... | collective-permute-start | bytes 57704 | tf_op jit(solution)/shard_map/ppermute | solution.py:24
  204.6 9.1 %collective-permute-start.7 = (bf16[1,16,601]{1,2,0:T(8,128)(2,1)}, bf16[1,16,601]{1,2,0:T(8,128)(2,1)}, u32[]{:S(2)}, u32[]{:S(2)}) collective-permute-start(bf16[1,16,601]{1,2,0:T(8,128)(2,1)} %collective-permute-done.6), channel_id=1, source_target_pairs={{0,2},{2,4},{4,6},{6,8},{8,10},{10,12},{12,14},{14,16},{16,18},{18... | collective-permute-start | bytes 57704 | tf_op jit(solution)/shard_map/ppermute | solution.py:22
  208.9 15.1 %copy-start.26 = (pred[8,3]{0,1:T(4,128)(4,1)S(1)}, pred[8,3]{0,1:T(4,128)(4,1)}, u32[]{:S(2)}) copy-start(pred[8,3]{0,1:T(4,128)(4,1)} %constant.165) | copy-start | bytes 76
  226.1 0.8 copy-start.10
  231.0 0.7 copy-start.1
  232.0 3.0 copy-start.33
  234.1 0.9 copy-start.12
  239.1 3.3 copy-start.13
  242.5 2.8 copy-start.31
  244.6 0.7 copy-start.5
  250.0 2.3 copy-start.7
  252.3 38.9 %reduce-scatter.14.cloned.1.call-start = ((), (), s32[]{:S(2)}) async-start(), calls=%async_computation.11 | async-start | bytes 3538944 | tf_op jit(solution)/shard_map/reduce_scatter | solution.py:223
  261.8 2.5 copy-start.3
  265.3 2.2 copy-start.17
  267.8 0.9 copy-start.4
  272.3 0.9 copy-start.8
  272.3 1.1 copy-start.11
  272.3 1.2 copy-start.19
  272.3 3.2 copy-start.6
  272.3 3.9 copy-start.16
  272.3 19.9 %reduce-scatter.10.cloned.1.call-start = ((), (), s32[]{:S(2)}) async-start(), calls=%async_computation.9 | async-start | bytes 3538944 | tf_op jit(solution)/shard_map/reduce_scatter | solution.py:222
  278.2 1.0 copy-start.2
  283.6 0.7 copy-start.37
  283.6 1.4 copy-start.32
  283.6 88.8 %reduce-scatter.22.cloned.1.call-start = ((), (), s32[]{:S(2)}) async-start(), calls=%async_computation.15 | async-start | bytes 139264
  286.2 87.0 %copy-start.29 = (f32[1,16]{1,0:T(1,128)S(1)}, f32[1,16]{1,0:T(1,128)}, u32[]{:S(2)}) copy-start(f32[1,16]{1,0:T(1,128)} %param.30) | copy-start | bytes 196
  286.2 87.0 %copy-start.30 = (f32[1,16]{1,0:T(1,128)S(1)}, f32[1,16]{1,0:T(1,128)}, u32[]{:S(2)}) copy-start(f32[1,16]{1,0:T(1,128)} %param.31) | copy-start | bytes 196
  286.2 163.2 %copy-start.18 = (f32[1,16,601]{2,1,0:T(8,128)S(1)}, f32[1,16,601]{2,1,0:T(8,128)}, u32[]{:S(2)}) copy-start(f32[1,16,601]{2,1,0:T(8,128)} %param.22) | copy-start | bytes 115396
  286.2 163.2 %copy-start.24 = (f32[1,16,601]{2,1,0:T(8,128)S(1)}, f32[1,16,601]{2,1,0:T(8,128)}, u32[]{:S(2)}) copy-start(f32[1,16,601]{2,1,0:T(8,128)} %param.28) | copy-start | bytes 115396
  286.2 163.2 %copy-start.25 = (f32[1,16,601]{2,1,0:T(8,128)S(1)}, f32[1,16,601]{2,1,0:T(8,128)}, u32[]{:S(2)}) copy-start(f32[1,16,601]{2,1,0:T(8,128)} %param.29) | copy-start | bytes 115396
  286.2 241.3 %copy-start.14 = (f32[3,3,16,128]{3,2,1,0:T(8,128)S(1)}, f32[3,3,16,128]{3,2,1,0:T(8,128)}, u32[]{:S(2)}) copy-start(f32[3,3,16,128]{3,2,1,0:T(8,128)} %param.21) | copy-start | bytes 221188
  286.3 241.3 %copy-start.20 = (f32[3,3,16,128]{3,2,1,0:T(8,128)S(1)}, f32[3,3,16,128]{3,2,1,0:T(8,128)}, u32[]{:S(2)}) copy-start(f32[3,3,16,128]{3,2,1,0:T(8,128)} %param.26) | copy-start | bytes 221188
  286.3 241.3 %copy-start.21 = (f32[3,3,16,128]{3,2,1,0:T(8,128)S(1)}, f32[3,3,16,128]{3,2,1,0:T(8,128)}, u32[]{:S(2)}) copy-start(f32[3,3,16,128]{3,2,1,0:T(8,128)} %param.27) | copy-start | bytes 221188
  286.3 319.7 %copy-start.15 = (f32[3,3,16,128]{3,2,1,0:T(8,128)S(1)}, f32[3,3,16,128]{3,2,1,0:T(8,128)}, u32[]{:S(2)}) copy-start(f32[3,3,16,128]{3,2,1,0:T(8,128)} %param.20) | copy-start | bytes 221188
  286.3 319.7 %copy-start.22 = (f32[3,3,16,128]{3,2,1,0:T(8,128)S(1)}, f32[3,3,16,128]{3,2,1,0:T(8,128)}, u32[]{:S(2)}) copy-start(f32[3,3,16,128]{3,2,1,0:T(8,128)} %param.24) | copy-start | bytes 221188
  286.3 319.7 %copy-start.23 = (f32[3,3,16,128]{3,2,1,0:T(8,128)S(1)}, f32[3,3,16,128]{3,2,1,0:T(8,128)}, u32[]{:S(2)}) copy-start(f32[3,3,16,128]{3,2,1,0:T(8,128)} %param.25) | copy-start | bytes 221188
  290.4 159.0 %reduce-scatter.20.cloned.1.call-start = ((), (), s32[]{:S(2)}) async-start(), calls=%async_computation.14 | async-start | bytes 696320 | tf_op jit(solution)/shard_map/reduce_scatter | solution.py:230
  291.2 236.3 %reduce-scatter.16.cloned.1.call-start = ((), (), s32[]{:S(2)}) async-start(), calls=%async_computation.12 | async-start | bytes 1253376 | tf_op jit(solution)/shard_map/reduce_scatter | solution.py:229
  291.9 314.0 %reduce-scatter.12.cloned.1.call-start = ((), (), s32[]{:S(2)}) async-start(), calls=%async_computation.10 | async-start | bytes 1253376 | tf_op jit(solution)/shard_map/reduce_scatter | solution.py:228
  373.2 234.4 %copy-start.27 = (f32[1,16]{1,0:T(1,128)}, f32[1,16]{1,0:T(1,128)S(1)}, u32[]{:S(2)}) copy-start(f32[1,16]{1,0:T(1,128)S(1)} %copy.89) | copy-start | bytes 196
Sparse Core Ops, SparseCore 0:
  56.8 4.7 all-gather.3
  105.9 6.2 all-gather.5
  252.5 5.2 reduce-scatter.17
  272.4 6.3 reduce-scatter.13
  283.7 8.4 reduce-scatter.9
  294.3 78.0 reduce-scatter.21
  375.2 74.1 reduce-scatter.19
  452.3 75.2 reduce-scatter.15
  530.4 75.5 reduce-scatter.11
